TPU v7x, 32 devices: a whole 2x2x4 slice. The times are simulated.
32 devices in a mesh: blk: 8 (over z, x), uly: 4 (over y, core).
Axes of the slice: x: 2, y: 2, z: 4, core: 2. Of those that a mesh axis runs over, the one named last changes fastest.
Arguments:
- q_raw: bfloat16 [1152, 24, 128], P('blk', 'uly'), may hold values from -120 to 120
- k_raw: bfloat16 [1152, 24, 128], P('blk', 'uly'), may hold values from -120 to 120
- values: bfloat16 [1152, 24, 128], P('blk', 'uly'), may hold values from -6 to 6
- out_grad: bfloat16 [1152, 24, 128], P('blk', 'uly'), may hold values from -16 to 16
- q_gain: float32 [2, 128], replicated, may hold values from 0.5 to 6.5
- k_gain: float32 [2, 128], replicated, may hold values from 0.5 to 6.5
Outputs:
- q_grad: bfloat16 [1152, 24, 128], P('blk', 'uly')
- k_grad: bfloat16 [1152, 24, 128], P('blk', 'uly')
- v_grad: bfloat16 [1152, 24, 128], P('blk', 'uly')
- q_gain_grad: float32 [2, 128], replicated
- k_gain_grad: float32 [2, 128], replicated
All inputs are finite; a program needn't handle non-finite values.
Results may differ from a plain program's by a relative error of at most 0.009.
The roundings to bfloat16 on the way count: a program that leaves them out, or rounds other values in their place, can miss the bound.
Values may be sent and summed in bfloat16 or wider, within the bound.
A program may use at most 64 MiB of HBM per device.

v0:
```python
import functools
import math

import jax
import jax.numpy as jnp
from jax import lax
from jax.experimental import pallas as pl
from jax.experimental.pallas import tpu as pltpu
from jax.sharding import PartitionSpec as P

TXT = 512
EPS = 1e-06
CHUNK = 128
MESH = pl.DeviceIdType.MESH
f32, bf16 = jnp.float32, jnp.bfloat16


def partner(me, step, n):
    if n & (n - 1):
        return (me + step) % n
    out, bit = 0, 1
    while bit < n:
        out = out + ((me // bit + step // bit) % 2) * bit
        bit *= 2
    return out


def kernel(
    n, n_uly, heads, rows,
    k_hbm, v_hbm, q_hbm, g_hbm, qg_ref, kg_ref,
    dq_out, dk_out, dv_out, q_gain_out, k_gain_out,
    k_in, v_in, q_in, g_in,
    k_all, v_all, q_all, g_all, kn, kn_t, dk_acc, dv_acc, dq_buf, dk_buf, dv_buf,
    gain_mine, gain_heads, gain_group, gain_uly,
    staged, in_send, in_recv, back_send, back_recv, g1_send, g1_recv, g2_send, g2_recv,
):
    me = lax.axis_index("blk")
    uly = lax.axis_index("uly")
    total = n * rows
    chunks = total // CHUNK
    width = k_in.shape[2]
    factor = 1.0 / math.sqrt(width)
    phase = (uly % 2) * (heads % n)

    def head_of(dev):
        return (heads * dev + phase) // n

    def owns(dev):
        return (heads * dev + phase) % n + heads >= n

    def owner(h):
        return ((h + 1) * n - phase + heads - 1) // heads - 1

    mine = head_of(me)
    i_own = owns(me)

    sources = (k_hbm, v_hbm, q_hbm, g_hbm)
    ins = (k_in, v_in, q_in, g_in)
    alls = (k_all, v_all, q_all, g_all)
    backs = (dq_buf, dk_buf, dv_buf)
    outs = (dq_out, dk_out, dv_out)

    def block(dev):
        return pl.ds(pl.multiple_of(dev * rows, 16), rows)

    def stage(a):
        return pltpu.make_async_copy(sources[a], ins[a], staged.at[a])

    for a in range(4):
        stage(a).start()

    barrier = pltpu.get_barrier_semaphore()
    for s in range(1, n):
        pl.semaphore_signal(
            barrier, inc=1, device_id={"blk": partner(me, s, n)}, device_id_type=MESH
        )
    for s in range(1, n_uly):
        pl.semaphore_signal(
            barrier, inc=1, device_id={"uly": (uly + s) % n_uly}, device_id_type=MESH
        )
    pl.semaphore_wait(barrier, n - 1 + n_uly - 1)

    def in_copy(a, s, h, dev):
        return pltpu.make_async_remote_copy(
            src_ref=ins[a].at[h], dst_ref=alls[a].at[block(me)],
            send_sem=in_send.at[a, s], recv_sem=in_recv.at[a, me],
            device_id={"blk": dev}, device_id_type=MESH,
        )

    def send_in(a, s):
        dev = partner(me, s, n)

        @pl.when(owns(dev))
        def _():
            in_copy(a, s, head_of(dev), dev).start()

    def keep_in(a):
        @pl.when(i_own)
        def _():
            pltpu.make_async_copy(
                ins[a].at[mine], alls[a].at[block(me)], in_recv.at[a, me]
            ).start()

    def wait_in(a, src):
        pltpu.make_async_copy(ins[a].at[0], alls[a].at[block(src)], in_recv.at[a, src]).wait()

    for a in (0, 1):
        stage(a).wait()
        for s in range(n - 1, 0, -1):
            send_in(a, s)
    for a in (2, 3):
        stage(a).wait()
    for a in range(4):
        keep_in(a)
    for s in range(1, n):
        for a in (2, 3):
            send_in(a, s)

    def back_copy(a, dev):
        return pltpu.make_async_remote_copy(
            src_ref=backs[a].at[block(dev)], dst_ref=outs[a].at[mine],
            send_sem=back_send.at[a, dev], recv_sem=back_recv.at[a, mine],
            device_id={"blk": dev}, device_id_type=MESH,
        )

    def send_back(a, dev):
        @pl.when(dev != me)
        def _():
            back_copy(a, dev).start()

        @pl.when(dev == me)
        def _():
            pltpu.make_async_copy(
                backs[a].at[block(dev)], outs[a].at[mine], back_recv.at[a, mine]
            ).start()

    def gains_at(gain_ref, base):
        position = base + lax.broadcasted_iota(jnp.int32, (CHUNK, width), 0)
        text = position < TXT
        return text, jnp.where(text, gain_ref[0:1, :], gain_ref[1:2, :])

    def unit_of(raw):
        wide = raw.astype(f32)
        inverse = lax.rsqrt(jnp.mean(wide * wide, axis=-1, keepdims=True) + EPS)
        return wide * inverse, inverse

    def finish(grad, unit, inverse, text, gains):
        part = grad * unit
        scaled = grad * gains
        text_sum = jnp.sum(jnp.where(text, part, 0.0), axis=0, keepdims=True)
        image_sum = jnp.sum(jnp.where(text, 0.0, part), axis=0, keepdims=True)
        result = (scaled - unit * jnp.mean(scaled * unit, axis=-1, keepdims=True)) * inverse
        return result.astype(bf16), text_sum, image_sum

    @pl.when(i_own)
    def _():
        low = me < n // 2
        turn = jnp.where(low, me, n - 1 - me) >= n // 4
        half = chunks // 2
        half_need = (CHUNK * half - 1) // rows + 1
        half_done = (CHUNK * half) // rows

        def real(i, count):
            return jnp.where(low, i, count - 1 - i)

        gain_mine[...] = jnp.zeros_like(gain_mine)
        dk_acc[...] = jnp.zeros_like(dk_acc)
        dv_acc[...] = jnp.zeros_like(dv_acc)

        @pl.loop(0, n)
        def _(src):
            wait_in(0, src)

        @pl.loop(0, chunks)
        def _(c):
            at = pl.ds(pl.multiple_of(c * CHUNK, CHUNK), CHUNK)
            text, gains = gains_at(kg_ref, c * CHUNK)
            unit, _inverse = unit_of(k_all[at, :])
            normed = unit * gains
            kn[at, :] = normed.astype(bf16)
            kn_t[:, at] = normed.T.astype(bf16)

        @pl.loop(0, n)
        def _(src):
            wait_in(1, src)

        @pl.loop(0, chunks)
        def _(i):
            down = jnp.logical_and(turn, i >= half)
            t = jnp.where(down, i - half, i)
            need = (CHUNK * (t + 1) - 1) // rows + 1
            had = jnp.where(t == 0, 0, (CHUNK * t - 1) // rows + 1)
            left = jnp.where(down, n - half_need, n)

            @pl.when(jnp.logical_and(need > had, had < left))
            def _():
                src = real(jnp.where(down, n - 1 - had, had), n)
                wait_in(2, src)
                wait_in(3, src)

            c = real(jnp.where(down, chunks - 1 - t, t), chunks)
            at = pl.ds(pl.multiple_of(c * CHUNK, CHUNK), CHUNK)
            text, gains = gains_at(qg_ref, c * CHUNK)
            unit, inverse = unit_of(q_all[at, :])
            qn = (unit * gains).astype(bf16)
            grads = g_all[at, :]
            nt = (((1,), (1,)), ((), ()))
            scores = lax.dot_general(kn[...], qn, nt, preferred_element_type=f32)
            peak = jnp.max(scores, axis=0, keepdims=True)
            weights = jnp.exp((scores - peak) * factor)
            probs = weights * (1.0 / jnp.sum(weights, axis=0, keepdims=True))
            grad_probs = lax.dot_general(v_all[...], grads, nt, preferred_element_type=f32)
            mixed = probs * grad_probs
            row_dot = jnp.sum(mixed, axis=0, keepdims=True)
            grad_scores = (probs * (grad_probs - row_dot)).astype(bf16)
            probs_low = probs.astype(bf16)
            dv_acc[...] += jnp.dot(probs_low, grads, preferred_element_type=f32)
            dk_acc[...] += jnp.dot(grad_scores, qn, preferred_element_type=f32)
            weighted_grad = jnp.dot(kn_t[...], mixed.astype(bf16), preferred_element_type=f32)
            weighted_keys = jnp.dot(kn_t[...], probs_low, preferred_element_type=f32)
            grad_q = ((weighted_grad - row_dot * weighted_keys) * factor).T
            result, text_sum, image_sum = finish(grad_q, unit, inverse, text, gains)
            dq_buf[at, :] = result
            gain_mine[0:1, :] += text_sum
            gain_mine[1:2, :] += image_sum

            done = (CHUNK * (t + 1)) // rows
            before = (CHUNK * t) // rows

            @pl.when(done > before)
            def _():
                send_back(0, real(jnp.where(down, n - 1 - before, before), n))

        if half_done + (CHUNK * (chunks - half)) // rows < n:
            @pl.when(turn)
            def _():
                send_back(0, real(half_done, n))

        dv_buf[...] = dv_acc[...].astype(bf16)

        def far_first(s):
            return partner(me, n - 1 - s, n) if n & (n - 1) == 0 else s

        @pl.loop(0, n)
        def _(s):
            send_back(2, far_first(s))

        @pl.loop(0, chunks)
        def _(c):
            at = pl.ds(pl.multiple_of(c * CHUNK, CHUNK), CHUNK)
            text, gains = gains_at(kg_ref, c * CHUNK)
            unit, inverse = unit_of(k_all[at, :])
            result, text_sum, image_sum = finish(
                dk_acc[at, :] * factor, unit, inverse, text, gains
            )
            dk_buf[at, :] = result
            gain_mine[2:3, :] += text_sum
            gain_mine[3:4, :] += image_sum

        def gain_copy(dev):
            return pltpu.make_async_remote_copy(
                src_ref=gain_mine, dst_ref=gain_heads.at[mine],
                send_sem=g1_send.at[dev], recv_sem=g1_recv.at[mine],
                device_id={"blk": dev}, device_id_type=MESH,
            )

        @pl.loop(1, n)
        def _(s):
            gain_copy(partner(me, s, n)).start()

        pltpu.make_async_copy(gain_mine, gain_heads.at[mine], g1_recv.at[mine]).start()

        @pl.loop(0, n)
        def _(s):
            send_back(1, far_first(s))

        @pl.loop(1, n)
        def _(s):
            dev = partner(me, s, n)
            gain_copy(dev).wait_send()

    for h in range(heads):
        pltpu.make_async_copy(gain_mine, gain_heads.at[h], g1_recv.at[h]).wait()
    group = gain_heads[0]
    for h in range(1, heads):
        group = group + gain_heads[h]
    gain_group[...] = group

    def uly_copy(s):
        return pltpu.make_async_remote_copy(
            src_ref=gain_group, dst_ref=gain_uly.at[uly],
            send_sem=g2_send.at[s], recv_sem=g2_recv.at[uly],
            device_id={"uly": (uly + s) % n_uly}, device_id_type=MESH,
        )

    for s in range(1, n_uly):
        uly_copy(s).start()
    gain_uly[uly] = group
    for s in range(1, n_uly):
        src = (uly + s) % n_uly
        pltpu.make_async_copy(gain_group, gain_uly.at[src], g2_recv.at[src]).wait()
    summed = gain_uly[0]
    for u in range(1, n_uly):
        summed = summed + gain_uly[u]
    q_gain_out[...] = summed[0:2, :]
    k_gain_out[...] = summed[2:4, :]

    for s in range(1, n_uly):
        uly_copy(s).wait_send()

    for a in range(3):
        for h in range(heads):
            pltpu.make_async_copy(
                backs[a].at[block(0)], outs[a].at[h], back_recv.at[a, h]
            ).wait()

    @pl.when(i_own)
    def _():
        @pl.loop(1, n)
        def _(s):
            dev = partner(me, s, n)
            for a in range(3):
                back_copy(a, dev).wait_send()

    @pl.loop(1, n)
    def _(s):
        dev = partner(me, s, n)

        @pl.when(owns(dev))
        def _():
            for a in range(4):
                in_copy(a, s, head_of(dev), dev).wait_send()


def store(*refs):
    count = len(refs) // 2
    sems = refs[-1]
    copies = [
        pltpu.make_async_copy(refs[i], refs[count + i], sems.at[i]) for i in range(count)
    ]
    for copy in copies:
        copy.start()
    for copy in copies:
        copy.wait()


def solution(mesh):
    n, n_uly = mesh.shape["blk"], mesh.shape["uly"]

    def local(q_raw, k_raw, values, out_grad, q_gain, k_gain):
        rows, heads, width = q_raw.shape
        total = n * rows
        vmem = pl.BlockSpec(memory_space=pltpu.VMEM)
        first = [jnp.transpose(x, (1, 0, 2)) for x in (k_raw, values, q_raw, out_grad)]
        out_block = jax.ShapeDtypeStruct((heads, rows, width), bf16)
        hbm = pl.BlockSpec(memory_space=pltpu.HBM)
        gain_block = jax.ShapeDtypeStruct((2, width), f32)
        shapes = (out_block,) * 3 + (gain_block,) * 2
        results = pl.pallas_call(
            functools.partial(kernel, n, n_uly, heads, rows),
            out_shape=shapes,
            in_specs=[hbm] * 4 + [vmem] * 2,
            out_specs=(vmem,) * 5,
            scratch_shapes=[pltpu.VMEM((heads, rows, width), bf16)] * 4
            + [pltpu.VMEM((total, width), bf16)] * 5
            + [pltpu.VMEM((width, total), bf16)]
            + [pltpu.VMEM((total, width), f32)] * 2
            + [pltpu.VMEM((total, width), bf16)] * 3
            + [
                pltpu.VMEM((8, width), f32),
                pltpu.VMEM((heads, 8, width), f32),
                pltpu.VMEM((8, width), f32),
                pltpu.VMEM((n_uly, 8, width), f32),
                pltpu.SemaphoreType.DMA((4,)),
                pltpu.SemaphoreType.DMA((4, n)),
                pltpu.SemaphoreType.DMA((4, n)),
                pltpu.SemaphoreType.DMA((3, n)),
                pltpu.SemaphoreType.DMA((3, heads)),
                pltpu.SemaphoreType.DMA((n,)),
                pltpu.SemaphoreType.DMA((heads,)),
                pltpu.SemaphoreType.DMA((n_uly,)),
                pltpu.SemaphoreType.DMA((n_uly,)),
            ],
            compiler_params=pltpu.CompilerParams(
                collective_id=0, has_side_effects=True, vmem_limit_bytes=67043328
            ),
        )(*first, q_gain, k_gain)
        dq, dk, dv, q_total, k_total = pl.pallas_call(
            store,
            out_shape=shapes,
            in_specs=[vmem] * 5,
            out_specs=(hbm,) * 5,
            scratch_shapes=[pltpu.SemaphoreType.DMA((5,))],
        )(*results)
        back = [jnp.transpose(x, (1, 0, 2)) for x in (dq, dk, dv)]
        return (*back, q_total, k_total)

    placed = (P("blk", "uly", None),) * 4 + (P(), P())
    return jax.shard_map(
        local,
        mesh=mesh,
        in_specs=placed,
        out_specs=(P("blk", "uly", None),) * 3 + (P(), P()),
        check_vma=False,
    )
```

profile of v0, /device:TPU:0, one launch (start us, length us, event | category | flops | bytes accessed | tf_op | source)
XLA Modules:
  0.0 51.2 jit_solution(7463152243953028322)
XLA Ops:
  0.6 48.6 %shard_map.101 = (bf16[6,144,128]{2,1,0:T(8,128)(2,1)}, bf16[6,144,128]{2,1,0:T(8,128)(2,1)}, bf16[6,144,128]{2,1,0:T(8,128)(2,1)}, f32[2,128]{1,0:T(2,128)}, f32[2,128]{1,0:T(2,128)}) custom-call(bf16[6,144,128]{2,1,0:T(8,128)(2,1)} %bitcast.7, bf16[6,144,128]{2,1,0:T(8,128)(2,1)} %bitcast.8, bf16[6,144,128]{2,1,0:T(8,128)(2,1)} %bitcast.9, ...), custom_call_target="tpu_custom_call" | custom-call | tf_op jit(solution)/shard_map/pallas_call | solution.py:359
  49.2 2.0 %shard_map.102 = (bf16[6,144,128]{2,1,0:T(8,128)(2,1)}, bf16[6,144,128]{2,1,0:T(8,128)(2,1)}, bf16[6,144,128]{2,1,0:T(8,128)(2,1)}, f32[2,128]{1,0:T(2,128)}, f32[2,128]{1,0:T(2,128)}) custom-call(bf16[6,144,128]{2,1,0:T(8,128)(2,1)} %get-tuple-element.15.refs_0_, bf16[6,144,128]{2,1,0:T(8,128)(2,1)} %get-tuple-element.16.refs_1_, ...), custom_call_target="tpu_custom_call" | custom-call | tf_op jit(solution)/shard_map/pallas_call | solution.py:388
where the time goes:
time: 51.4 us; the launch traced here: 51.2 us
  Pallas kernels  50.6 us (98%)
  between operations  0.64 us (1%)
    pallas_call x1, Pallas kernels, local(): pl.pallas_call(functools.partial(kernel, n, n_uly, heads, rows), out_shap...  48.6 us
    pallas_call x1, Pallas kernels, local(): pl.pallas_call(store, out_shape=shapes, in_specs=[vmem] * 5, out_specs=(h...  2.03 us

commit v1 on v0

--- a/solution.py
+++ b/solution.py
@@ -10,7 +10,9 @@
 
 TXT = 512
 EPS = 1e-06
-CHUNK = 128
+LANES = 128
+CHUNK = 256
+KEYS = 1152
 MESH = pl.DeviceIdType.MESH
 f32, bf16 = jnp.float32, jnp.bfloat16
 
@@ -27,19 +29,24 @@
 
 def kernel(
     n, n_uly, heads, rows,
-    k_hbm, v_hbm, q_hbm, g_hbm, qg_ref, kg_ref,
+    k_hbm, v_hbm, q_hbm, g_hbm, qg_hbm, kg_hbm,
     dq_out, dk_out, dv_out, q_gain_out, k_gain_out,
     k_in, v_in, q_in, g_in,
     k_all, v_all, q_all, g_all, kn, kn_t, dk_acc, dv_acc, dq_buf, dk_buf, dv_buf,
-    gain_mine, gain_heads, gain_group, gain_uly,
+    weights_buf, grad_buf, low_buf, mixed_buf, scores_grad_buf, peaks, sums, dots, scales,
+    qg_ref, kg_ref, gain_mine, gain_heads, gain_group, gain_uly,
     staged, in_send, in_recv, back_send, back_recv, g1_send, g1_recv, g2_send, g2_recv,
 ):
     me = lax.axis_index("blk")
     uly = lax.axis_index("uly")
     total = n * rows
-    chunks = total // CHUNK
+    full = total // CHUNK
+    tail = total - full * CHUNK
+    tiles = total // LANES
     width = k_in.shape[2]
     factor = 1.0 / math.sqrt(width)
+    factor2 = factor * math.log2(math.e)
+    keys = max(d for d in range(LANES, min(total, KEYS) + 1, LANES) if total % d == 0)
     phase = (uly % 2) * (heads % n)
 
     def head_of(dev):
@@ -66,8 +73,10 @@
     def stage(a):
         return pltpu.make_async_copy(sources[a], ins[a], staged.at[a])
 
-    for a in range(4):
-        stage(a).start()
+    gain_stages = (
+        pltpu.make_async_copy(qg_hbm, qg_ref, staged.at[4]),
+        pltpu.make_async_copy(kg_hbm, kg_ref, staged.at[5]),
+    )
 
     barrier = pltpu.get_barrier_semaphore()
     for s in range(1, n):
@@ -78,6 +87,10 @@
         pl.semaphore_signal(
             barrier, inc=1, device_id={"uly": (uly + s) % n_uly}, device_id_type=MESH
         )
+    for a in range(4):
+        stage(a).start()
+    for copy in gain_stages:
+        copy.start()
     pl.semaphore_wait(barrier, n - 1 + n_uly - 1)
 
     def in_copy(a, s, h, dev):
@@ -110,6 +123,8 @@
             send_in(a, s)
     for a in (2, 3):
         stage(a).wait()
+    for copy in gain_stages:
+        copy.wait()
     for a in range(4):
         keep_in(a)
     for s in range(1, n):
@@ -134,8 +149,22 @@
                 backs[a].at[block(dev)], outs[a].at[mine], back_recv.at[a, mine]
             ).start()
 
-    def gains_at(gain_ref, base):
-        position = base + lax.broadcasted_iota(jnp.int32, (CHUNK, width), 0)
+    def gain_copy(dev):
+        return pltpu.make_async_remote_copy(
+            src_ref=gain_mine, dst_ref=gain_heads.at[mine],
+            send_sem=g1_send.at[dev], recv_sem=g1_recv.at[mine],
+            device_id={"blk": dev}, device_id_type=MESH,
+        )
+
+    def uly_copy(s):
+        return pltpu.make_async_remote_copy(
+            src_ref=gain_group, dst_ref=gain_uly.at[uly],
+            send_sem=g2_send.at[s], recv_sem=g2_recv.at[uly],
+            device_id={"uly": (uly + s) % n_uly}, device_id_type=MESH,
+        )
+
+    def gains_at(gain_ref, base, size):
+        position = base + lax.broadcasted_iota(jnp.int32, (size, width), 0)
         text = position < TXT
         return text, jnp.where(text, gain_ref[0:1, :], gain_ref[1:2, :])
 
@@ -156,9 +185,11 @@
     def _():
         low = me < n // 2
         turn = jnp.where(low, me, n - 1 - me) >= n // 4
-        half = chunks // 2
+        half = full // 2
         half_need = (CHUNK * half - 1) // rows + 1
         half_done = (CHUNK * half) // rows
+        rest_done = (CHUNK * (full - half)) // rows
+        nt = (((1,), (1,)), ((), ()))
 
         def real(i, count):
             return jnp.where(low, i, count - 1 - i)
@@ -171,10 +202,10 @@
         def _(src):
             wait_in(0, src)
 
-        @pl.loop(0, chunks)
+        @pl.loop(0, tiles)
         def _(c):
-            at = pl.ds(pl.multiple_of(c * CHUNK, CHUNK), CHUNK)
-            text, gains = gains_at(kg_ref, c * CHUNK)
+            at = pl.ds(pl.multiple_of(c * LANES, LANES), LANES)
+            text, gains = gains_at(kg_ref, c * LANES, LANES)
             unit, _inverse = unit_of(k_all[at, :])
             normed = unit * gains
             kn[at, :] = normed.astype(bf16)
@@ -184,71 +215,134 @@
         def _(src):
             wait_in(1, src)
 
-        @pl.loop(0, chunks)
-        def _(i):
-            down = jnp.logical_and(turn, i >= half)
-            t = jnp.where(down, i - half, i)
-            need = (CHUNK * (t + 1) - 1) // rows + 1
-            had = jnp.where(t == 0, 0, (CHUNK * t - 1) // rows + 1)
-            left = jnp.where(down, n - half_need, n)
-
-            @pl.when(jnp.logical_and(need > had, had < left))
-            def _():
-                src = real(jnp.where(down, n - 1 - had, had), n)
-                wait_in(2, src)
-                wait_in(3, src)
-
-            c = real(jnp.where(down, chunks - 1 - t, t), chunks)
-            at = pl.ds(pl.multiple_of(c * CHUNK, CHUNK), CHUNK)
-            text, gains = gains_at(qg_ref, c * CHUNK)
+        def over_keys(body):
+            if keys == total:
+                body(0)
+            else:
+                @pl.loop(0, total // keys)
+                def _(j):
+                    body(j)
+
+        def attend(start, size):
+            start = pl.multiple_of(start, LANES)
+            at = pl.ds(start, size)
+            text, gains = gains_at(qg_ref, start, size)
             unit, inverse = unit_of(q_all[at, :])
             qn = (unit * gains).astype(bf16)
             grads = g_all[at, :]
-            nt = (((1,), (1,)), ((), ()))
-            scores = lax.dot_general(kn[...], qn, nt, preferred_element_type=f32)
-            peak = jnp.max(scores, axis=0, keepdims=True)
-            weights = jnp.exp((scores - peak) * factor)
-            probs = weights * (1.0 / jnp.sum(weights, axis=0, keepdims=True))
-            grad_probs = lax.dot_general(v_all[...], grads, nt, preferred_element_type=f32)
-            mixed = probs * grad_probs
-            row_dot = jnp.sum(mixed, axis=0, keepdims=True)
-            grad_scores = (probs * (grad_probs - row_dot)).astype(bf16)
-            probs_low = probs.astype(bf16)
-            dv_acc[...] += jnp.dot(probs_low, grads, preferred_element_type=f32)
-            dk_acc[...] += jnp.dot(grad_scores, qn, preferred_element_type=f32)
-            weighted_grad = jnp.dot(kn_t[...], mixed.astype(bf16), preferred_element_type=f32)
-            weighted_keys = jnp.dot(kn_t[...], probs_low, preferred_element_type=f32)
+            cols = pl.ds(0, size)
+            per = keys // LANES
+
+            def first(j):
+                base = pl.multiple_of(j * keys, LANES)
+                rng = pl.ds(base, keys)
+                scores = lax.dot_general(kn[rng, :], qn, nt, preferred_element_type=f32)
+                grad_probs = lax.dot_general(v_all[rng, :], grads, nt, preferred_element_type=f32)
+                for b in range(per):
+                    part = slice(b * LANES, (b + 1) * LANES)
+                    here = pl.ds(base + b * LANES, LANES)
+                    row = pl.ds(j * per + b, 1)
+                    peak = jnp.max(scores[part], axis=0, keepdims=True)
+                    weights = jnp.exp2((scores[part] - peak) * factor2)
+                    peaks[row, cols] = peak
+                    sums[row, cols] = jnp.sum(weights, axis=0, keepdims=True)
+                    dots[row, cols] = jnp.sum(weights * grad_probs[part], axis=0, keepdims=True)
+                    weights_buf[here, cols] = weights
+                    grad_buf[here, cols] = grad_probs[part]
+
+            over_keys(first)
+            peak_all = peaks[:, cols]
+            lift = jnp.exp2((peak_all - jnp.max(peak_all, axis=0, keepdims=True)) * factor2)
+            inverse_total = 1.0 / jnp.sum(lift * sums[:, cols], axis=0, keepdims=True)
+            row_dot = jnp.sum(lift * dots[:, cols], axis=0, keepdims=True) * inverse_total
+            scales[:, cols] = lift * inverse_total
+
+            def second(j):
+                base = pl.multiple_of(j * keys, LANES)
+                rng = pl.ds(base, keys)
+                for b in range(per):
+                    here = pl.ds(base + b * LANES, LANES)
+                    row = pl.ds(j * per + b, 1)
+                    probs = weights_buf[here, cols] * scales[row, cols]
+                    grad_probs = grad_buf[here, cols]
+                    low_buf[here, cols] = probs.astype(bf16)
+                    mixed_buf[here, cols] = (probs * grad_probs).astype(bf16)
+                    scores_grad_buf[here, cols] = (probs * (grad_probs - row_dot)).astype(bf16)
+                dv_acc[rng, :] += jnp.dot(low_buf[rng, cols], grads, preferred_element_type=f32)
+                dk_acc[rng, :] += jnp.dot(
+                    scores_grad_buf[rng, cols], qn, preferred_element_type=f32
+                )
+
+            over_keys(second)
+            weighted_grad = jnp.dot(kn_t[...], mixed_buf[:, cols], preferred_element_type=f32)
+            weighted_keys = jnp.dot(kn_t[...], low_buf[:, cols], preferred_element_type=f32)
             grad_q = ((weighted_grad - row_dot * weighted_keys) * factor).T
             result, text_sum, image_sum = finish(grad_q, unit, inverse, text, gains)
             dq_buf[at, :] = result
             gain_mine[0:1, :] += text_sum
             gain_mine[1:2, :] += image_sum
 
-            done = (CHUNK * (t + 1)) // rows
-            before = (CHUNK * t) // rows
-
-            @pl.when(done > before)
+        def send_range(begin, end, flip):
+            @pl.loop(begin, end)
+            def _(k):
+                send_back(0, real(jnp.where(flip, n - 1 - k, k), n))
+
+        def place(i):
+            down = jnp.logical_and(turn, i >= half)
+            return down, jnp.where(down, i - half, i)
+
+        def send_done(i):
+            down, t = place(i)
+            send_range((CHUNK * t) // rows, (CHUNK * (t + 1)) // rows, down)
+
+        @pl.loop(0, full)
+        def _(i):
+            down, t = place(i)
+            need = (CHUNK * (t + 1) - 1) // rows + 1
+            had = jnp.where(t == 0, 0, (CHUNK * t - 1) // rows + 1)
+            need = jnp.where(down, jnp.minimum(need, n - half_need), need)
+
+            @pl.loop(had, need)
+            def _(k):
+                src = real(jnp.where(down, n - 1 - k, k), n)
+                wait_in(2, src)
+                wait_in(3, src)
+
+            @pl.when(i == full - 1)
             def _():
-                send_back(0, real(jnp.where(down, n - 1 - before, before), n))
-
-        if half_done + (CHUNK * (chunks - half)) // rows < n:
-            @pl.when(turn)
+                @pl.loop(0, full - 1)
+                def _(k):
+                    send_done(k)
+
+            begin = jnp.where(down, total - CHUNK * (t + 1), CHUNK * t)
+            attend(jnp.where(low, begin, total - CHUNK - begin), CHUNK)
+            @pl.when(i == full - 1)
             def _():
-                send_back(0, real(half_done, n))
-
-        dv_buf[...] = dv_acc[...].astype(bf16)
-
-        def far_first(s):
-            return partner(me, n - 1 - s, n) if n & (n - 1) == 0 else s
-
-        @pl.loop(0, n)
-        def _(s):
-            send_back(2, far_first(s))
-
-        @pl.loop(0, chunks)
+                send_done(i)
+
+        if tail:
+            had_all = (CHUNK * full - 1) // rows + 1
+            left_had = (CHUNK * (full - half) - 1) // rows + 1
+            seen = jnp.where(turn, jnp.minimum(half_need + left_had, n), had_all)
+
+            @pl.loop(seen, n)
+            def _(k):
+                k = jnp.where(turn, half_need + k - seen, k)
+                wait_in(2, real(k, n))
+                wait_in(3, real(k, n))
+
+            begin = jnp.where(turn, CHUNK * half, CHUNK * full)
+            attend(jnp.where(low, begin, total - tail - begin), tail)
+        send_range(
+            jnp.where(turn, half_done, (CHUNK * full) // rows),
+            jnp.where(turn, n - rest_done, n),
+            False,
+        )
+
+        @pl.loop(0, tiles)
         def _(c):
-            at = pl.ds(pl.multiple_of(c * CHUNK, CHUNK), CHUNK)
-            text, gains = gains_at(kg_ref, c * CHUNK)
+            at = pl.ds(pl.multiple_of(c * LANES, LANES), LANES)
+            text, gains = gains_at(kg_ref, c * LANES, LANES)
             unit, inverse = unit_of(k_all[at, :])
             result, text_sum, image_sum = finish(
                 dk_acc[at, :] * factor, unit, inverse, text, gains
@@ -257,27 +351,24 @@
             gain_mine[2:3, :] += text_sum
             gain_mine[3:4, :] += image_sum
 
-        def gain_copy(dev):
-            return pltpu.make_async_remote_copy(
-                src_ref=gain_mine, dst_ref=gain_heads.at[mine],
-                send_sem=g1_send.at[dev], recv_sem=g1_recv.at[mine],
-                device_id={"blk": dev}, device_id_type=MESH,
-            )
-
         @pl.loop(1, n)
         def _(s):
             gain_copy(partner(me, s, n)).start()
 
         pltpu.make_async_copy(gain_mine, gain_heads.at[mine], g1_recv.at[mine]).start()
 
+        dv_buf[...] = dv_acc[...].astype(bf16)
+
+        def far_first(s):
+            return jnp.where(low, n - 1 - s, s)
+
+        @pl.loop(0, n)
+        def _(s):
+            send_back(2, far_first(s))
+
         @pl.loop(0, n)
         def _(s):
             send_back(1, far_first(s))
-
-        @pl.loop(1, n)
-        def _(s):
-            dev = partner(me, s, n)
-            gain_copy(dev).wait_send()
 
     for h in range(heads):
         pltpu.make_async_copy(gain_mine, gain_heads.at[h], g1_recv.at[h]).wait()
@@ -285,14 +376,6 @@
     for h in range(1, heads):
         group = group + gain_heads[h]
     gain_group[...] = group
-
-    def uly_copy(s):
-        return pltpu.make_async_remote_copy(
-            src_ref=gain_group, dst_ref=gain_uly.at[uly],
-            send_sem=g2_send.at[s], recv_sem=g2_recv.at[uly],
-            device_id={"uly": (uly + s) % n_uly}, device_id_type=MESH,
-        )
-
     for s in range(1, n_uly):
         uly_copy(s).start()
     gain_uly[uly] = group
@@ -316,6 +399,10 @@
 
     @pl.when(i_own)
     def _():
+        @pl.loop(1, n)
+        def _(s):
+            gain_copy(partner(me, s, n)).wait_send()
+
         @pl.loop(1, n)
         def _(s):
             dev = partner(me, s, n)
@@ -359,19 +446,24 @@
         results = pl.pallas_call(
             functools.partial(kernel, n, n_uly, heads, rows),
             out_shape=shapes,
-            in_specs=[hbm] * 4 + [vmem] * 2,
+            in_specs=[hbm] * 6,
             out_specs=(vmem,) * 5,
             scratch_shapes=[pltpu.VMEM((heads, rows, width), bf16)] * 4
             + [pltpu.VMEM((total, width), bf16)] * 5
             + [pltpu.VMEM((width, total), bf16)]
             + [pltpu.VMEM((total, width), f32)] * 2
             + [pltpu.VMEM((total, width), bf16)] * 3
+            + [pltpu.VMEM((total, CHUNK), f32)] * 2
+            + [pltpu.VMEM((total, CHUNK), bf16)] * 3
+            + [pltpu.VMEM((total // LANES, CHUNK), f32)] * 4
             + [
-                pltpu.VMEM((8, width), f32),
-                pltpu.VMEM((heads, 8, width), f32),
-                pltpu.VMEM((8, width), f32),
-                pltpu.VMEM((n_uly, 8, width), f32),
-                pltpu.SemaphoreType.DMA((4,)),
+                pltpu.VMEM((2, width), f32),
+                pltpu.VMEM((2, width), f32),
+                pltpu.VMEM((4, width), f32),
+                pltpu.VMEM((heads, 4, width), f32),
+                pltpu.VMEM((4, width), f32),
+                pltpu.VMEM((n_uly, 4, width), f32),
+                pltpu.SemaphoreType.DMA((6,)),
                 pltpu.SemaphoreType.DMA((4, n)),
                 pltpu.SemaphoreType.DMA((4, n)),
                 pltpu.SemaphoreType.DMA((3, n)),

time: 51.4 us -> 47.6 us (0.926)
  Pallas kernels: 50.6 us -> 46.8 us
    pallas_call x1, Pallas kernels: 48.6 us -> 44.8 us  [local(): pl.pallas_call(functools.partial(kernel, n, n_uly, heads, rows), out_shap...]
where the time goes in v1:
time: 47.6 us; the launch traced here: 47.4 us
  Pallas kernels  46.8 us (98%)
  between operations  0.64 us (1%)
    pallas_call x1, Pallas kernels, local(): pl.pallas_call(functools.partial(kernel, n, n_uly, heads, rows), out_shap...  44.8 us
    pallas_call x1, Pallas kernels, local(): pl.pallas_call(store, out_shape=shapes, in_specs=[vmem] * 5, out_specs=(h...  2.03 us

profile of v1, /device:TPU:0, one launch (start us, length us, event | category | flops | bytes accessed | tf_op | source)
XLA Modules:
  0.0 47.4 jit_solution(3140690588372787401)
XLA Ops:
  0.6 44.8 %shard_map.101 = (bf16[6,144,128]{2,1,0:T(8,128)(2,1)}, bf16[6,144,128]{2,1,0:T(8,128)(2,1)}, bf16[6,144,128]{2,1,0:T(8,128)(2,1)}, f32[2,128]{1,0:T(2,128)}, f32[2,128]{1,0:T(2,128)}) custom-call(bf16[6,144,128]{2,1,0:T(8,128)(2,1)} %bitcast.7, bf16[6,144,128]{2,1,0:T(8,128)(2,1)} %bitcast.8, bf16[6,144,128]{2,1,0:T(8,128)(2,1)} %bitcast.9, ...), custom_call_target="tpu_custom_call" | custom-call | tf_op jit(solution)/shard_map/pallas_call | solution.py:446
  45.4 2.0 %shard_map.102 = (bf16[6,144,128]{2,1,0:T(8,128)(2,1)}, bf16[6,144,128]{2,1,0:T(8,128)(2,1)}, bf16[6,144,128]{2,1,0:T(8,128)(2,1)}, f32[2,128]{1,0:T(2,128)}, f32[2,128]{1,0:T(2,128)}) custom-call(bf16[6,144,128]{2,1,0:T(8,128)(2,1)} %get-tuple-element.15.refs_0_, bf16[6,144,128]{2,1,0:T(8,128)(2,1)} %get-tuple-element.16.refs_1_, ...), custom_call_target="tpu_custom_call" | custom-call | tf_op jit(solution)/shard_map/pallas_call | solution.py:480

commit v2 on v1

--- a/solution.py
+++ b/solution.py
@@ -13,6 +13,8 @@
 LANES = 128
 CHUNK = 256
 KEYS = 1152
+KERNEL_VMEM = 48 * 2**20
+STORE_VMEM = 2**20
 MESH = pl.DeviceIdType.MESH
 f32, bf16 = jnp.float32, jnp.bfloat16
 
@@ -443,9 +445,10 @@
         hbm = pl.BlockSpec(memory_space=pltpu.HBM)
         gain_block = jax.ShapeDtypeStruct((2, width), f32)
         shapes = (out_block,) * 3 + (gain_block,) * 2
+        held = tuple(pltpu.VMEM(x.shape, x.dtype) for x in shapes)
         results = pl.pallas_call(
             functools.partial(kernel, n, n_uly, heads, rows),
-            out_shape=shapes,
+            out_shape=held,
             in_specs=[hbm] * 6,
             out_specs=(vmem,) * 5,
             scratch_shapes=[pltpu.VMEM((heads, rows, width), bf16)] * 4
@@ -474,15 +477,16 @@
                 pltpu.SemaphoreType.DMA((n_uly,)),
             ],
             compiler_params=pltpu.CompilerParams(
-                collective_id=0, has_side_effects=True, vmem_limit_bytes=67043328
+                collective_id=0, has_side_effects=True, vmem_limit_bytes=KERNEL_VMEM
             ),
-        )(*first, q_gain, k_gain)
+        )(*[pltpu.with_memory_space_constraint(x, pltpu.HBM) for x in (*first, q_gain, k_gain)])
         dq, dk, dv, q_total, k_total = pl.pallas_call(
             store,
             out_shape=shapes,
             in_specs=[vmem] * 5,
             out_specs=(hbm,) * 5,
             scratch_shapes=[pltpu.SemaphoreType.DMA((5,))],
+            compiler_params=pltpu.CompilerParams(vmem_limit_bytes=STORE_VMEM),
         )(*results)
         back = [jnp.transpose(x, (1, 0, 2)) for x in (dq, dk, dv)]
         return (*back, q_total, k_total)

time: 47.6 us -> 45.6 us (0.958)
  Pallas kernels: 46.8 us -> 44.8 us
    pallas_call x1, Pallas kernels: 2.03 us -> 0.88 us  [local(): pl.pallas_call(store, out_shape=shapes, in_specs=[vmem] * 5, out_specs=(h...]
    pallas_call x1, Pallas kernels: 44.8 us -> 43.9 us  [local(): pl.pallas_call(functools.partial(kernel, n, n_uly, heads, rows), out_shap...]
where the time goes in v2:
time: 45.6 us; the launch traced here: 45.5 us
  Pallas kernels  44.8 us (98%)
  between operations  0.64 us (1%)
    pallas_call x1, Pallas kernels, local(): pl.pallas_call(functools.partial(kernel, n, n_uly, heads, rows), out_shap...  43.9 us

profile of v2, /device:TPU:0, one launch (start us, length us, event | category | flops | bytes accessed | tf_op | source)
XLA Modules:
  0.0 45.5 jit_solution(1024404531732792084)
XLA Ops:
  0.6 43.9 %shard_map.101 = (bf16[6,144,128]{2,1,0:T(8,128)(2,1)S(1)}, bf16[6,144,128]{2,1,0:T(8,128)(2,1)S(1)}, bf16[6,144,128]{2,1,0:T(8,128)(2,1)S(1)}, f32[2,128]{1,0:T(2,128)S(1)}, f32[2,128]{1,0:T(2,128)S(1)}) custom-call(bf16[6,144,128]{2,1,0:T(8,128)(2,1)} %bitcast.7, bf16[6,144,128]{2,1,0:T(8,128)(2,1)} %bitcast.8, bf16[6,144,128]{2,1,0:T(8,128)(2,1)} %bitcast.9, ...), custom_call_target="tpu_custom_call" | custom-call | tf_op jit(solution)/shard_map/pallas_call | solution.py:449
  44.6 0.9 %shard_map.102 = (bf16[6,144,128]{2,1,0:T(8,128)(2,1)}, bf16[6,144,128]{2,1,0:T(8,128)(2,1)}, bf16[6,144,128]{2,1,0:T(8,128)(2,1)}, f32[2,128]{1,0:T(2,128)}, f32[2,128]{1,0:T(2,128)}) custom-call(bf16[6,144,128]{2,1,0:T(8,128)(2,1)S(1)} %get-tuple-element.15.refs_0_, bf16[6,144,128]{2,1,0:T(8,128)(2,1)S(1)} %get-tuple-element.16.refs_1_, ...), custom_call_target="tpu_custom_call" | custom-call | tf_op jit(solution)/shard_map/pallas_call | solution.py:483

commit v3 on v2

--- a/solution.py
+++ b/solution.py
@@ -37,7 +37,7 @@
     k_all, v_all, q_all, g_all, kn, kn_t, dk_acc, dv_acc, dq_buf, dk_buf, dv_buf,
     weights_buf, grad_buf, low_buf, mixed_buf, scores_grad_buf, peaks, sums, dots, scales,
     qg_ref, kg_ref, gain_mine, gain_heads, gain_group, gain_uly,
-    staged, in_send, in_recv, back_send, back_recv, g1_send, g1_recv, g2_send, g2_recv,
+    staged, in_send, in_recv, back_send, back_recv, g1_send, g1_recv, g2_send, g2_recv, entered,
 ):
     me = lax.axis_index("blk")
     uly = lax.axis_index("uly")
@@ -80,20 +80,54 @@
         pltpu.make_async_copy(kg_hbm, kg_ref, staged.at[5]),
     )
 
+    quarter = n // 4
+
+    def inner(dev):
+        return jnp.logical_and(dev >= quarter, dev < n - quarter)
+
+    i_inner = inner(me)
+    pair = jnp.where((me // quarter) % 2 == 0, me + quarter, me - quarter)
     barrier = pltpu.get_barrier_semaphore()
-    for s in range(1, n):
-        pl.semaphore_signal(
-            barrier, inc=1, device_id={"blk": partner(me, s, n)}, device_id_type=MESH
-        )
     for s in range(1, n_uly):
         pl.semaphore_signal(
             barrier, inc=1, device_id={"uly": (uly + s) % n_uly}, device_id_type=MESH
         )
+
+    @pl.when(i_inner)
+    def _():
+        @pl.loop(quarter, n - quarter)
+        def _(dev):
+            @pl.when(dev != me)
+            def _():
+                pl.semaphore_signal(barrier, inc=1, device_id={"blk": dev}, device_id_type=MESH)
+
     for a in range(4):
         stage(a).start()
     for copy in gain_stages:
         copy.start()
-    pl.semaphore_wait(barrier, n - 1 + n_uly - 1)
+
+    @pl.when(i_inner)
+    def _():
+        pl.semaphore_wait(barrier, n - 2 * quarter - 1 + n_uly - 1)
+        pl.semaphore_signal(barrier, inc=1, device_id={"blk": pair}, device_id_type=MESH)
+
+    @pl.when(jnp.logical_not(i_inner))
+    def _():
+        pl.semaphore_wait(barrier, 1 + n_uly - 1)
+
+        @pl.loop(quarter, n - quarter)
+        def _(dev):
+            pl.semaphore_signal(entered, inc=1, device_id={"blk": dev}, device_id_type=MESH)
+
+    def meet():
+        @pl.when(i_inner)
+        def _():
+            pl.semaphore_wait(entered, 2 * quarter)
+            pl.semaphore_signal(entered, inc=1, device_id={"blk": pair}, device_id_type=MESH)
+
+        @pl.when(jnp.logical_not(i_inner))
+        def _():
+            pl.semaphore_wait(entered, 1)
 
     def in_copy(a, s, h, dev):
         return pltpu.make_async_remote_copy(
@@ -102,10 +136,13 @@
             device_id={"blk": dev}, device_id_type=MESH,
         )
 
-    def send_in(a, s):
+    def send_in(a, s, near=None):
         dev = partner(me, s, n)
-
-        @pl.when(owns(dev))
+        wanted = owns(dev)
+        if near is not None:
+            wanted = jnp.logical_and(wanted, inner(dev) == near)
+
+        @pl.when(wanted)
         def _():
             in_copy(a, s, head_of(dev), dev).start()
 
@@ -119,10 +156,14 @@
     def wait_in(a, src):
         pltpu.make_async_copy(ins[a].at[0], alls[a].at[block(src)], in_recv.at[a, src]).wait()
 
-    for a in (0, 1):
-        stage(a).wait()
-        for s in range(n - 1, 0, -1):
-            send_in(a, s)
+    for first in (True, False):
+        for a in (0, 1):
+            if first:
+                stage(a).wait()
+            for s in range(n - 1, 0, -1):
+                send_in(a, s, first)
+        if first:
+            meet()
     for a in (2, 3):
         stage(a).wait()
     for copy in gain_stages:
@@ -475,6 +516,7 @@
                 pltpu.SemaphoreType.DMA((heads,)),
                 pltpu.SemaphoreType.DMA((n_uly,)),
                 pltpu.SemaphoreType.DMA((n_uly,)),
+                pltpu.SemaphoreType.REGULAR,
             ],
             compiler_params=pltpu.CompilerParams(
                 collective_id=0, has_side_effects=True, vmem_limit_bytes=KERNEL_VMEM

time: 45.6 us -> 44.8 us (0.982)
  Pallas kernels: 44.8 us -> 44 us
    pallas_call x1, Pallas kernels: 43.9 us -> 43.1 us  [local(): pl.pallas_call(functools.partial(kernel, n, n_uly, heads, rows), out_shap...]
where the time goes in v3:
time: 44.8 us; the launch traced here: 44.6 us
  Pallas kernels  44 us (98%)
  between operations  0.64 us (1%)
    pallas_call x1, Pallas kernels, local(): pl.pallas_call(functools.partial(kernel, n, n_uly, heads, rows), out_shap...  43.1 us

profile of v3, /device:TPU:0, one launch (start us, length us, event | category | flops | bytes accessed | tf_op | source)
XLA Modules:
  0.0 44.6 jit_solution(10242596346000306761)
XLA Ops:
  0.6 43.1 %shard_map.101 = (bf16[6,144,128]{2,1,0:T(8,128)(2,1)S(1)}, bf16[6,144,128]{2,1,0:T(8,128)(2,1)S(1)}, bf16[6,144,128]{2,1,0:T(8,128)(2,1)S(1)}, f32[2,128]{1,0:T(2,128)S(1)}, f32[2,128]{1,0:T(2,128)S(1)}) custom-call(bf16[6,144,128]{2,1,0:T(8,128)(2,1)} %bitcast.7, bf16[6,144,128]{2,1,0:T(8,128)(2,1)} %bitcast.8, bf16[6,144,128]{2,1,0:T(8,128)(2,1)} %bitcast.9, ...), custom_call_target="tpu_custom_call" | custom-call | tf_op jit(solution)/shard_map/pallas_call | solution.py:490
  43.7 0.9 %shard_map.102 = (bf16[6,144,128]{2,1,0:T(8,128)(2,1)}, bf16[6,144,128]{2,1,0:T(8,128)(2,1)}, bf16[6,144,128]{2,1,0:T(8,128)(2,1)}, f32[2,128]{1,0:T(2,128)}, f32[2,128]{1,0:T(2,128)}) custom-call(bf16[6,144,128]{2,1,0:T(8,128)(2,1)S(1)} %get-tuple-element.15.refs_0_, bf16[6,144,128]{2,1,0:T(8,128)(2,1)S(1)} %get-tuple-element.16.refs_1_, ...), custom_call_target="tpu_custom_call" | custom-call | tf_op jit(solution)/shard_map/pallas_call | solution.py:525

commit v4 on v3

--- a/solution.py
+++ b/solution.py
@@ -45,6 +45,7 @@
     full = total // CHUNK
     tail = total - full * CHUNK
     tiles = total // LANES
+    unroll = max(u for u in range(1, 10) if tiles % u == 0)
     width = k_in.shape[2]
     factor = 1.0 / math.sqrt(width)
     factor2 = factor * math.log2(math.e)
@@ -245,7 +246,7 @@
         def _(src):
             wait_in(0, src)
 
-        @pl.loop(0, tiles)
+        @pl.loop(0, tiles, unroll=unroll)
         def _(c):
             at = pl.ds(pl.multiple_of(c * LANES, LANES), LANES)
             text, gains = gains_at(kg_ref, c * LANES, LANES)
@@ -382,7 +383,7 @@
             False,
         )
 
-        @pl.loop(0, tiles)
+        @pl.loop(0, tiles, unroll=unroll)
         def _(c):
             at = pl.ds(pl.multiple_of(c * LANES, LANES), LANES)
             text, gains = gains_at(kg_ref, c * LANES, LANES)
@@ -402,16 +403,36 @@
 
         dv_buf[...] = dv_acc[...].astype(bf16)
 
-        def far_first(s):
-            return jnp.where(low, n - 1 - s, s)
-
-        @pl.loop(0, n)
+        side = n // 2
+
+        def spread(j):
+            return jnp.where(j < quarter, 2 * j, 2 * (j - quarter) + 1)
+
+        def target(s):
+            crossing = jnp.logical_and(s > 0, s <= side)
+            ahead = jnp.where(crossing, side + spread(s - 1), spread(s % side))
+            behind = jnp.where(s < side, spread(s), side + spread(s - side))
+            return jnp.where(low, ahead, behind)
+
+        for a in (2, 1):
+            send_back(a, target(0))
+
+        @pl.loop(1, n)
         def _(s):
-            send_back(2, far_first(s))
-
-        @pl.loop(0, n)
+            send_back(2, target(s))
+
+        @pl.loop(1, n)
         def _(s):
-            send_back(1, far_first(s))
+            send_back(1, target(s))
+
+    @pl.loop(1, n)
+    def _(s):
+        dev = partner(me, s, n)
+
+        @pl.when(owns(dev))
+        def _():
+            for a in range(4):
+                in_copy(a, s, head_of(dev), dev).wait_send()
 
     for h in range(heads):
         pltpu.make_async_copy(gain_mine, gain_heads.at[h], g1_recv.at[h]).wait()
@@ -434,11 +455,12 @@
     for s in range(1, n_uly):
         uly_copy(s).wait_send()
 
-    for a in range(3):
+    def wait_back(a):
         for h in range(heads):
-            pltpu.make_async_copy(
-                backs[a].at[block(0)], outs[a].at[h], back_recv.at[a, h]
-            ).wait()
+            pltpu.make_async_copy(backs[a].at[block(0)], outs[a].at[h], back_recv.at[a, h]).wait()
+
+    wait_back(0)
+    wait_back(2)
 
     @pl.when(i_own)
     def _():
@@ -452,14 +474,7 @@
             for a in range(3):
                 back_copy(a, dev).wait_send()
 
-    @pl.loop(1, n)
-    def _(s):
-        dev = partner(me, s, n)
-
-        @pl.when(owns(dev))
-        def _():
-            for a in range(4):
-                in_copy(a, s, head_of(dev), dev).wait_send()
+    wait_back(1)
 
 
 def store(*refs):

time: 44.8 us -> 43.3 us (0.967); the launches traced: 44.6 us -> 42.6 us
  Pallas kernels: 44 us -> 42 us
    pallas_call x1, Pallas kernels: 43.1 us -> 41.1 us  [local(): pl.pallas_call(functools.partial(kernel, n, n_uly, heads, rows), out_shap...]
where the time goes in v4:
time: 43.3 us; the launch traced here: 42.6 us
  Pallas kernels  42 us (97%)
  between operations  0.64 us (1%)
    pallas_call x1, Pallas kernels, local(): pl.pallas_call(functools.partial(kernel, n, n_uly, heads, rows), out_shap...  41.1 us
    pallas_call x1, Pallas kernels, local(): pl.pallas_call(store, out_shape=shapes, in_specs=[vmem] * 5, out_specs=(h...  0.88 us

profile of v4, /device:TPU:0, one launch (start us, length us, event | category | flops | bytes accessed | tf_op | source)
XLA Modules:
  0.0 42.6 jit_solution(8862383769816375105)
XLA Ops:
  0.6 41.1 %shard_map.101 = (bf16[6,144,128]{2,1,0:T(8,128)(2,1)S(1)}, bf16[6,144,128]{2,1,0:T(8,128)(2,1)S(1)}, bf16[6,144,128]{2,1,0:T(8,128)(2,1)S(1)}, f32[2,128]{1,0:T(2,128)S(1)}, f32[2,128]{1,0:T(2,128)S(1)}) custom-call(bf16[6,144,128]{2,1,0:T(8,128)(2,1)} %bitcast.7, bf16[6,144,128]{2,1,0:T(8,128)(2,1)} %bitcast.8, bf16[6,144,128]{2,1,0:T(8,128)(2,1)} %bitcast.9, ...), custom_call_target="tpu_custom_call" | custom-call | tf_op jit(solution)/shard_map/pallas_call | solution.py:505
  41.7 0.9 %shard_map.102 = (bf16[6,144,128]{2,1,0:T(8,128)(2,1)}, bf16[6,144,128]{2,1,0:T(8,128)(2,1)}, bf16[6,144,128]{2,1,0:T(8,128)(2,1)}, f32[2,128]{1,0:T(2,128)}, f32[2,128]{1,0:T(2,128)}) custom-call(bf16[6,144,128]{2,1,0:T(8,128)(2,1)S(1)} %get-tuple-element.15.refs_0_, bf16[6,144,128]{2,1,0:T(8,128)(2,1)S(1)} %get-tuple-element.16.refs_1_, ...), custom_call_target="tpu_custom_call" | custom-call | tf_op jit(solution)/shard_map/pallas_call | solution.py:540

commit v5 on v4

--- a/solution.py
+++ b/solution.py
@@ -50,16 +50,16 @@
     factor = 1.0 / math.sqrt(width)
     factor2 = factor * math.log2(math.e)
     keys = max(d for d in range(LANES, min(total, KEYS) + 1, LANES) if total % d == 0)
-    phase = (uly % 2) * (heads % n)
+    def rank(dev):
+        side = n // 2
+        turned = jnp.where(dev < side, dev, n - 1 + side - dev)
+        return jnp.where(uly % 2 == 0, turned, turned + 1 - 2 * (turned % 2))
 
     def head_of(dev):
-        return (heads * dev + phase) // n
+        return (heads * rank(dev)) // n
 
     def owns(dev):
-        return (heads * dev + phase) % n + heads >= n
-
-    def owner(h):
-        return ((h + 1) * n - phase + heads - 1) // heads - 1
+        return (heads * rank(dev)) % n + heads >= n
 
     mine = head_of(me)
     i_own = owns(me)
@@ -411,8 +411,7 @@
         def target(s):
             crossing = jnp.logical_and(s > 0, s <= side)
             ahead = jnp.where(crossing, side + spread(s - 1), spread(s % side))
-            behind = jnp.where(s < side, spread(s), side + spread(s - side))
-            return jnp.where(low, ahead, behind)
+            return jnp.where(low, ahead, s)
 
         for a in (2, 1):
             send_back(a, target(0))

time: 43.3 us -> 42.8 us (0.988)
  Pallas kernels: 42 us -> 41.4 us
    pallas_call x1, Pallas kernels: 41.1 us -> 40.5 us  [local(): pl.pallas_call(functools.partial(kernel, n, n_uly, heads, rows), out_shap...]
where the time goes in v5:
time: 42.8 us; the launch traced here: 42 us
  Pallas kernels  41.4 us (97%)
  between operations  0.64 us (1%)
    pallas_call x1, Pallas kernels, local(): pl.pallas_call(functools.partial(kernel, n, n_uly, heads, rows), out_shap...  40.5 us
    pallas_call x1, Pallas kernels, local(): pl.pallas_call(store, out_shape=shapes, in_specs=[vmem] * 5, out_specs=(h...  0.88 us

profile of v5, /device:TPU:0, one launch (start us, length us, event | category | flops | bytes accessed | tf_op | source)
XLA Modules:
  0.0 42.0 jit_solution(13188707166608071733)
XLA Ops:
  0.6 40.5 %shard_map.101 = (bf16[6,144,128]{2,1,0:T(8,128)(2,1)S(1)}, bf16[6,144,128]{2,1,0:T(8,128)(2,1)S(1)}, bf16[6,144,128]{2,1,0:T(8,128)(2,1)S(1)}, f32[2,128]{1,0:T(2,128)S(1)}, f32[2,128]{1,0:T(2,128)S(1)}) custom-call(bf16[6,144,128]{2,1,0:T(8,128)(2,1)} %bitcast.7, bf16[6,144,128]{2,1,0:T(8,128)(2,1)} %bitcast.8, bf16[6,144,128]{2,1,0:T(8,128)(2,1)} %bitcast.9, ...), custom_call_target="tpu_custom_call" | custom-call | tf_op jit(solution)/shard_map/pallas_call | solution.py:504
  41.1 0.9 %shard_map.102 = (bf16[6,144,128]{2,1,0:T(8,128)(2,1)}, bf16[6,144,128]{2,1,0:T(8,128)(2,1)}, bf16[6,144,128]{2,1,0:T(8,128)(2,1)}, f32[2,128]{1,0:T(2,128)}, f32[2,128]{1,0:T(2,128)}) custom-call(bf16[6,144,128]{2,1,0:T(8,128)(2,1)S(1)} %get-tuple-element.15.refs_0_, bf16[6,144,128]{2,1,0:T(8,128)(2,1)S(1)} %get-tuple-element.16.refs_1_, ...), custom_call_target="tpu_custom_call" | custom-call | tf_op jit(solution)/shard_map/pallas_call | solution.py:539
